TPU v7x, 256 devices: a 4x2x16 block of a 4x16x16 slice. The times are simulated.
256 devices in a mesh: groups: 2 (over y), lon: 128 (over z, x, core).
Axes of the slice: x: 4, y: 2, z: 16, core: 2. Of those that a mesh axis runs over, the one named last changes fastest.
The devices are a block of a 4x16x16 slice.
Arguments:
- tokens: bfloat16 [8, 24, 768, 512], P('groups', None, 'lon'), parts along dimension 0, may hold values from -6 to 6
- window_shift: int32 [2, 3], replicated, may hold values from 0 to 11, as said below
- fine_gain: float32 [512], replicated, may hold values from 0.25 to 1.75
- fine_qkv: bfloat16 [512, 1536], replicated
- fine_proj: bfloat16 [512, 512], replicated, may hold values from -0.25 to 0.25
- merge_gain: float32 [2048], replicated, may hold values from 0.25 to 1.75
- merge_weight: bfloat16 [2048, 512], replicated, may hold values from -0.125 to 0.125
- coarse_gain: float32 [512], replicated, may hold values from 0.25 to 1.75
- coarse_qkv: bfloat16 [512, 1536], replicated
- coarse_proj: bfloat16 [512, 512], replicated, may hold values from -0.25 to 0.25
- expand_weight: bfloat16 [512, 2048], replicated, may hold values from -0.25 to 0.25
- expand_gain: float32 [512], replicated, may hold values from 0.25 to 1.75
Outputs:
- forecast_state: bfloat16 [8, 24, 768, 512], P('groups', None, 'lon'), parts along dimension 0
There are 2 independent parts, one for each index of `groups`. A program takes and returns all parts, laid end to end along the dimension named above; an argument that names none is the same for every part. Nothing has to cross between parts.
Inputs may be any that keep to these rules, and one draw needn't show every extreme that they name: window_shift[k] holds offsets 0 to 1, 0 to 5 and 0 to 11 along level, latitude and longitude.
All inputs are finite; a program needn't handle non-finite values.
Results may differ from a plain program's by a relative error of at most 0.013.
Values may be sent and summed in bfloat16 or wider, within the bound.
A program may use at most 128 MiB of HBM per device.

v0:
```python
import math

import jax
import jax.numpy as jnp
from jax import lax
from jax.sharding import PartitionSpec as P

HEADS = 8
HC = 8
WIN_LEV = 2
WIN_LAT = 6
WIN_LON = 12


EPSILON = 1e-05


def passed_along(value, axis, steps):
    count = lax.axis_size(axis)
    pairs = [(source, (source + steps) % count) for source in range(count)]
    return lax.ppermute(value, axis, pairs)


def layer_norm(inputs, gain_vec):
    inputs = inputs.astype(jnp.float32)
    center = inputs - jnp.mean(inputs, axis=-1, keepdims=True)
    spread = jnp.mean(center * center, axis=-1, keepdims=True)
    return center * lax.rsqrt(spread + EPSILON) * gain_vec


def rolled_ids(length, offset, extent):
    placed = jnp.arange(length, dtype=jnp.int32)
    source = (placed - offset) % length
    return (source + offset) // extent


def roll_grid(tensor_in, offsets, factor):
    return jnp.roll(jnp.roll(tensor_in, factor * offsets[0], 0), factor * offsets[1], 1)


def window_attention(
    queries, key_block, value_block, query_cols, key_cols, offsets, lon_total, head_count
):
    levels, lat_rows, query_wide, features = queries.shape
    key_wide = key_block.shape[2]
    head_size = features // head_count
    lev_blocks = levels // WIN_LEV
    lat_blocks = lat_rows // WIN_LAT

    def blocked(tensor_in, wide_cols):
        tensor_in = tensor_in.reshape(
            lev_blocks, WIN_LEV, lat_blocks, WIN_LAT, wide_cols, head_count, head_size
        )
        tensor_in = tensor_in.transpose(0, 2, 1, 3, 4, 5, 6)
        return tensor_in.reshape(
            lev_blocks * lat_blocks, WIN_LEV * WIN_LAT * wide_cols, head_count, head_size
        )

    lev_ids = rolled_ids(levels, offsets[0], WIN_LEV).reshape(lev_blocks, WIN_LEV)
    row_ids = rolled_ids(lat_rows, offsets[1], WIN_LAT).reshape(lat_blocks, WIN_LAT)
    lev_same = lev_ids[:, :, None] == lev_ids[:, None, :]
    row_same = row_ids[:, :, None] == row_ids[:, None, :]
    query_win = (query_cols + offsets[2]) % lon_total // WIN_LON
    key_win = (key_cols + offsets[2]) % lon_total // WIN_LON
    col_same = query_win[:, None] == key_win[None, :]
    allowed = (
        lev_same[:, None, :, None, None, :, None, None]
        & row_same[None, :, None, :, None, None, :, None]
        & col_same[None, None, None, None, :, None, None, :]
    )
    allowed = allowed.reshape(
        lev_blocks * lat_blocks, WIN_LEV * WIN_LAT * query_wide, WIN_LEV * WIN_LAT * key_wide
    )
    query_b = blocked(queries, query_wide)
    key_b = blocked(key_block, key_wide)
    value_b = blocked(value_block, key_wide)
    scores = jnp.einsum(
        "bqhd,bkhd->bhqk", query_b, key_b, preferred_element_type=jnp.float32
    ) / math.sqrt(head_size)
    scores = jnp.where(allowed[:, None], scores, -1e30)
    row_max = jnp.max(scores, axis=-1, keepdims=True)
    expo = jnp.exp(scores - row_max)
    weight = (expo / jnp.sum(expo, axis=-1, keepdims=True)).astype(jnp.bfloat16)
    mixture = jnp.einsum(
        "bhqk,bkhd->bqhd", weight, value_b, preferred_element_type=jnp.float32
    ).astype(jnp.bfloat16)
    mixture = mixture.reshape(lev_blocks, lat_blocks, WIN_LEV, WIN_LAT, query_wide, features)
    return mixture.transpose(0, 2, 1, 3, 4, 5).reshape(levels, lat_rows, query_wide, features)


def widen(pieces, reach_cols, hop_size, sender):
    lon_cols = pieces.shape[2]
    distance_max = (reach_cols + lon_cols - 1) // lon_cols
    left_parts = []
    right_parts = []
    for distance in range(1, distance_max + 1):
        needed = min(lon_cols, reach_cols - (distance - 1) * lon_cols)
        for direction in (1, -1):
            portion = pieces[:, :, lon_cols - needed :] if direction > 0 else pieces[:, :, :needed]
            arrived = sender(portion, direction * distance * hop_size)
            if direction > 0:
                left_parts.insert(0, arrived)
            else:
                right_parts.append(arrived)
    return jnp.concatenate(left_parts + [pieces] + right_parts, axis=2)


def finish_block(grid, outputs, offsets, proj_weight):
    outputs = roll_grid(outputs, offsets, -1)
    update = jnp.dot(outputs, proj_weight, preferred_element_type=jnp.float32)
    return (grid.astype(jnp.float32) + update).astype(jnp.bfloat16)


def local(
    tokens,
    window_shift,
    fine_gain,
    fine_qkv,
    fine_proj,
    merge_gain,
    merge_weight,
    coarse_gain,
    coarse_qkv,
    coarse_proj,
    expand_weight,
    expand_gain,
):
    devices = lax.axis_size("lon")
    position = lax.axis_index("lon")
    levels, lat_rows, lon_cols, features = tokens.shape
    reach = WIN_LON - 1
    fine_offsets = window_shift[0]
    lon_total = devices * lon_cols
    normed = layer_norm(tokens, fine_gain).astype(jnp.bfloat16)
    wide_normed = widen(
        normed, reach, 1, lambda portion, stride: passed_along(portion, "lon", stride)
    )
    queries = jnp.dot(normed, fine_qkv[:, :features], preferred_element_type=jnp.float32).astype(
        jnp.bfloat16
    )
    wide_kv = jnp.dot(
        wide_normed, fine_qkv[:, features:], preferred_element_type=jnp.float32
    ).astype(jnp.bfloat16)
    first_col = position * lon_cols
    query_cols = first_col + jnp.arange(lon_cols, dtype=jnp.int32)
    key_cols = (first_col - reach + jnp.arange(lon_cols + 2 * reach, dtype=jnp.int32)) % lon_total
    queries = roll_grid(queries, fine_offsets, 1)
    wide_kv = roll_grid(wide_kv, fine_offsets, 1)
    outputs = window_attention(
        queries,
        wide_kv[..., :features],
        wide_kv[..., features:],
        query_cols,
        key_cols,
        fine_offsets,
        lon_total,
        HEADS,
    )
    fine = finish_block(tokens, outputs, fine_offsets, fine_proj)
    grouped = fine.reshape(levels, lat_rows // 2, 2, lon_cols // 2, 2, features)
    grouped = grouped.transpose(0, 1, 3, 4, 2, 5).reshape(
        levels, lat_rows // 2, lon_cols // 2, 4 * features
    )
    merged = layer_norm(grouped, merge_gain).astype(jnp.bfloat16)
    coarse = jnp.dot(merged, merge_weight, preferred_element_type=jnp.float32).astype(jnp.bfloat16)
    coarse_offsets = window_shift[1]
    channels = coarse.shape[-1]
    coarse_cols = lon_cols // 2
    coarse_total = devices * coarse_cols
    coarse_normed = layer_norm(coarse, coarse_gain).astype(jnp.bfloat16)
    coarse_projected = jnp.dot(
        coarse_normed, coarse_qkv, preferred_element_type=jnp.float32
    ).astype(jnp.bfloat16)
    coarse_queries = coarse_projected[..., :channels]
    own_kv = coarse_projected[..., channels:]
    coarse_query_cols = position * coarse_cols + jnp.arange(coarse_cols, dtype=jnp.int32)
    coarse_wide = widen(
        own_kv, reach, 1, lambda portion, stride: passed_along(portion, "lon", stride)
    )
    coarse_key_cols = (
        position * coarse_cols - reach + jnp.arange(coarse_cols + 2 * reach, dtype=jnp.int32)
    ) % coarse_total
    coarse_queries = roll_grid(coarse_queries, coarse_offsets, 1)
    coarse_wide = roll_grid(coarse_wide, coarse_offsets, 1)
    coarse_outputs = window_attention(
        coarse_queries,
        coarse_wide[..., :channels],
        coarse_wide[..., channels:],
        coarse_query_cols,
        coarse_key_cols,
        coarse_offsets,
        coarse_total,
        HC,
    )
    coarse_out = finish_block(coarse, coarse_outputs, coarse_offsets, coarse_proj)
    expanded = jnp.dot(coarse_out, expand_weight, preferred_element_type=jnp.float32)
    expanded = layer_norm(
        expanded.reshape(levels, lat_rows // 2, coarse_cols, 2, 2, features), expand_gain
    )
    expanded = expanded.transpose(0, 1, 4, 2, 3, 5).reshape(levels, lat_rows, lon_cols, features)
    return (fine.astype(jnp.float32) + expanded).astype(jnp.bfloat16)


def solution(mesh):
    placed = (P("groups", None, "lon", None), P(), P(), P(), P(), P(), P(), P(), P(), P(), P(), P())
    return jax.shard_map(
        local, mesh=mesh, in_specs=placed, out_specs=P("groups", None, "lon", None), check_vma=False
    )
```

profile of v0, /device:TPU:34, one launch (start us, length us, event | category | flops | bytes accessed | tf_op | source)
XLA Modules:
  0.0 248.8 jit_solution(1487799845601973111)
XLA Ops:
  0.0 1.4 convert_reduce_fusion
  1.4 1.4 fusion.41
  2.8 2.1 fusion.43
  4.9 1.7 collective-permute-start.2
  6.7 2.3 fusion.114
  9.0 1.6 collective-permute-start
  10.6 21.7 %collective-permute-start.3 = (bf16[4,24,5,512]{3,1,2,0:T(8,128)(2,1)}, bf16[4,24,5,512]{3,1,2,0:T(8,128)(2,1)}, u32[]{:S(2)}, u32[]{:S(2)}) collective-permute-start(bf16[4,24,5,512]{3,1,2,0:T(8,128)(2,1)} %get-tuple-element.15), channel_id=1, source_target_pairs={{0,126},{1,127},{2,0},{3,1},{4,2},{5,3},{6,4},{7,5},{8,6},{9,7},{1... | collective-permute-start | bytes 1474568 | tf_op jit(solution)/shard_map/ppermute | solution.py:21
  37.3 1.3 and_select_fusion.7
  43.0 2.5 %convolution_convert_fusion.2 = bf16[4,24,6,512]{3,1,2,0:T(8,128)(2,1)} fusion(bf16[4,24,6,512]{3,1,2,0:T(8,128)(2,1)} %fusion.43, bf16[512,1536]{1,0:T(8,128)(2,1)} %param.23), kind=kOutput, calls=%fused_computation.50 | convolution fusion | flops 302284800 | bytes 1703936 | tf_op jit(solution)/shard_map/dot_general | solution.py:138
  51.0 2.1 and.332
  53.5 1.3 fusion.64
  55.4 1.6 reshape.528
  57.0 2.6 %copy.165 = bf16[2,4,2,6,6,8,64]{6,5,4,3,2,1,0:T(8,128)(2,1)} copy(bf16[2,4,2,6,6,8,64]{6,5,3,1,4,2,0:T(8,128)(2,1)} %bitcast.121) | data formatting | bytes 1179648 | tf_op jit(solution)/shard_map/transpose | solution.py:54
  60.2 1.1 constant_dynamic-update-slice_fusion.4
  61.3 1.2 constant_dynamic-update-slice_fusion.3
  62.8 1.1 constant_dynamic-update-slice_fusion.1
  64.0 1.1 constant_dynamic-update-slice_fusion
  65.0 3.7 %convolution_convert_fusion = bf16[4,24,28,1024]{3,2,1,0:T(8,128)(2,1)S(1)} fusion(bf16[4,24,28,512]{3,1,2,0:T(8,128)(2,1)S(1)} %constant_dynamic-update-slice_fusion, bf16[512,1536]{1,0:T(8,128)(2,1)S(1)} %copy-done.19), kind=kOutput, calls=%fused_computation.23 | convolution fusion | flops 2821324800 | bytes 9306112 | tf_op jit(solution)/shard_map/dot_general | solution.py:141
  68.7 2.5 %fusion.3 = bf16[4,24,28,1024]{3,2,1,0:T(8,128)(2,1)S(1)} fusion(s32[]{:T(128)S(6)} %select_n.276, bf16[4,24,28,1024]{3,2,1,0:T(8,128)(2,1)S(1)} %convolution_convert_fusion), kind=kLoop, calls=%fused_computation.12 | loop fusion | flops 2752512 | bytes 11010052 | tf_op jit(solution)/shard_map/jit(_roll_dynamic)/concatenate | solution.py:38
  71.3 2.5 %fusion.2 = bf16[4,24,28,1024]{3,2,1,0:T(8,128)(2,1)S(1)} fusion(s32[]{:T(128)S(6)} %select_n.278, bf16[4,24,28,1024]{3,2,1,0:T(8,128)(2,1)S(1)} %fusion.3), kind=kLoop, calls=%fused_computation.11 | loop fusion | flops 2752512 | bytes 11010052 | tf_op jit(solution)/shard_map/jit(_roll_dynamic)/concatenate | solution.py:38
  73.8 2.6 %fusion.111 = (bf16[4,24,28,512]{3,2,1,0:T(8,128)(2,1)}, bf16[4,24,28,512]{3,2,1,0:T(8,128)(2,1)S(1)}) fusion(bf16[4,24,28,1024]{3,2,1,0:T(8,128)(2,1)S(1)} %fusion.2), kind=kLoop, calls=%fused_computation.200 | loop fusion | bytes 11010048 | tf_op jit(solution)/shard_map/slice | solution.py:152
  76.4 3.1 %copy.166 = bf16[4,24,28,512]{3,1,2,0:T(8,128)(2,1)} copy(bf16[4,24,28,512]{3,2,1,0:T(8,128)(2,1)S(1)} %get-tuple-element.8) | data formatting | bytes 5505024 | tf_op jit(solution)/shard_map/slice | solution.py:151
  79.4 8.2 %reshape.530 = bf16[2,2,4,6,28,8,64]{6,5,3,2,4,1,0:T(8,128)(2,1)} reshape(bf16[4,24,28,512]{3,1,2,0:T(8,128)(2,1)} %copy.166) | data formatting | bytes 5505024 | tf_op jit(solution)/shard_map/reshape | solution.py:51
  87.6 6.5 %copy.167 = bf16[2,4,2,6,28,8,64]{6,5,4,3,2,1,0:T(8,128)(2,1)} copy(bf16[2,4,2,6,28,8,64]{6,5,3,1,4,2,0:T(8,128)(2,1)} %bitcast.112) | data formatting | bytes 5505024 | tf_op jit(solution)/shard_map/transpose | solution.py:54
  94.2 3.2 %copy.163 = bf16[4,24,28,512]{3,1,2,0:T(8,128)(2,1)} copy(bf16[4,24,28,512]{3,2,1,0:T(8,128)(2,1)S(1)} %copy-done.1) | data formatting | bytes 5505024 | tf_op jit(solution)/shard_map/slice | solution.py:152
  97.4 7.8 %reshape.526 = bf16[2,2,4,6,28,8,64]{6,5,3,2,4,1,0:T(8,128)(2,1)} reshape(bf16[4,24,28,512]{3,1,2,0:T(8,128)(2,1)} %copy.163) | data formatting | bytes 5505024 | tf_op jit(solution)/shard_map/reshape | solution.py:51
  105.1 4.1 %copy.164 = bf16[2,4,2,6,28,8,64]{6,5,4,3,2,1,0:T(8,128)(2,1)S(1)} copy(bf16[2,4,2,6,28,8,64]{6,5,3,1,4,2,0:T(8,128)(2,1)} %bitcast.113) | data formatting | bytes 5505024 | tf_op jit(solution)/shard_map/transpose | solution.py:54
  109.7 2.0 fusion.6
  111.7 4.9 %fusion.116 = (f32[8,8,72]{2,1,0:T(8,128)S(1)}, f32[8,8,72,336]{3,2,1,0:T(8,128)}) fusion(f32[8,8,72,336]{3,2,1,0:T(8,128)S(1)} %fusion.6, pred[8,72,336]{2,1,0:T(8,128)(4,1)S(1)} %broadcast_and_fusion), kind=kOutput, calls=%fused_computation.205 | output fusion | flops 9290063 | bytes 12598272 | tf_op jit(solution)/shard_map/sub | solution.py:82
  116.5 6.3 %fusion.30 = bf16[8,72,8,64]{1,3,2,0:T(8,128)(2,1)} fusion(f32[8,8,72,336]{3,2,1,0:T(8,128)} %get-tuple-element.24, f32[8,8,72]{2,1,0:T(8,128)S(1)} %get-tuple-element.23, bf16[8,336,8,64]{3,2,1,0:T(8,128)(2,1)S(1)} %bitcast.120), kind=kOutput, calls=%fused_computation.47 | convolution fusion | flops 201572352 | bytes 9553920 | tf_op jit(solution)/shard_map/bhqk,bkhd->bqhd/dot_general | solution.py:84
  122.9 3.5 %copy.171 = bf16[8,72,8,64]{3,2,0,1:T(8,128)(2,1)} copy(bf16[8,72,8,64]{1,3,2,0:T(8,128)(2,1)} %fusion.30) | data formatting | bytes 1179648 | tf_op jit(solution)/shard_map/convert_element_type | solution.py:86
  126.4 2.9 %reshape.532 = bf16[2,4,2,6,6,512]{5,1,0,4,3,2:T(4,128)(2,1)} reshape(bf16[8,72,8,64]{3,2,0,1:T(8,128)(2,1)} %copy.171) | data formatting | bytes 1179648 | tf_op jit(solution)/shard_map/reshape | solution.py:87
  129.3 1.4 copy.214
  130.7 1.0 reshape.555
  131.7 1.3 fusion.62
  133.0 1.7 fusion.34
  134.7 1.1 copy-done.5
  136.6 2.0 copy.176
  139.7 2.5 %reshape.544 = f32[4,12,3,2048]{3,0,2,1:T(4,128)S(1)} reshape(f32[4,12,3,2,2,512]{5,4,3,0,2,1:T(2,128)} %copy.176) | data formatting | bytes 2359296 | tf_op jit(solution)/shard_map/convert_element_type | solution.py:25
  142.7 2.5 %fusion.117 = (f32[4,12,3]{1,2,0:T(4,128)S(1)}, f32[4,12,3,512]{3,1,2,0:T(8,128)S(1)}) fusion(bf16[2048,512]{1,0:T(8,128)(2,1)} %param.26, bf16[4,12,3,2048]{3,0,2,1:T(4,128)(2,1)S(1)} %multiply_convert_fusion), kind=kOutput, calls=%fused_computation.206 | convolution fusion | flops 302210944 | bytes 2982464 | tf_op jit(solution)/shard_map/dot_general | solution.py:165
  147.4 1.7 collective-permute-start.8
  150.9 30.3 %collective-permute-done.4 = bf16[4,12,2,1024]{3,1,2,0:T(8,128)(2,1)} collective-permute-done((bf16[4,12,2,1024]{3,1,2,0:T(8,128)(2,1)}, bf16[4,12,2,1024]{3,1,2,0:T(8,128)(2,1)}, u32[]{:S(2)}, u32[]{:S(2)}) %collective-permute-start.4) | collective-permute-done | bytes 196640 | tf_op jit(solution)/shard_map/ppermute | solution.py:21
  181.2 1.0 constant_dynamic-update-slice_fusion.13
  182.2 4.2 %collective-permute-start.10 = (bf16[4,12,3,1024]{3,1,2,0:T(8,128)(2,1)S(1)}, bf16[4,12,3,1024]{3,1,2,0:T(8,128)(2,1)S(1)}, u32[]{:S(2)}, u32[]{:S(2)}) collective-permute-start(bf16[4,12,3,1024]{3,1,2,0:T(8,128)(2,1)S(1)} %slice.107), channel_id=1, source_target_pairs={{0,125},{1,126},{2,127},{3,0},{4,1},{5,2},{6,3},{7,4},{8,5},{9,6},... | collective-permute-start | bytes 884744 | tf_op jit(solution)/shard_map/ppermute | solution.py:21
  186.4 1.0 constant_dynamic-update-slice_fusion.12
  187.4 5.5 %collective-permute-start.11 = (bf16[4,12,2,1024]{3,1,2,0:T(8,128)(2,1)}, bf16[4,12,2,1024]{3,1,2,0:T(8,128)(2,1)S(1)}, u32[]{:S(2)}, u32[]{:S(2)}) collective-permute-start(bf16[4,12,2,1024]{3,1,2,0:T(8,128)(2,1)} %get-tuple-element.13), channel_id=1, source_target_pairs={{0,124},{1,125},{2,126},{3,127},{4,0},{5,1},{6,2},{7,3},{8,4},{9,5... | collective-permute-start | bytes 589832 | tf_op jit(solution)/shard_map/ppermute | solution.py:21
  192.9 1.0 constant_dynamic-update-slice_fusion.11
  194.0 1.0 constant_dynamic-update-slice_fusion.10
  195.1 1.0 constant_dynamic-update-slice_fusion.8
  196.1 12.3 %collective-permute-done.10 = bf16[4,12,3,1024]{3,1,2,0:T(8,128)(2,1)S(1)} collective-permute-done((bf16[4,12,3,1024]{3,1,2,0:T(8,128)(2,1)S(1)}, bf16[4,12,3,1024]{3,1,2,0:T(8,128)(2,1)S(1)}, u32[]{:S(2)}, u32[]{:S(2)}) %collective-permute-start.10) | collective-permute-done | bytes 294944 | tf_op jit(solution)/shard_map/ppermute | solution.py:21
  208.5 1.4 fusion.13
  209.9 3.2 %fusion.12 = bf16[4,12,25,1024]{3,1,2,0:T(8,128)(2,1)S(1)} fusion(s32[]{:T(128)S(6)} %select_n.292, bf16[4,12,25,1024]{3,1,2,0:T(8,128)(2,1)S(1)} %fusion.13), kind=kLoop, calls=%fused_computation.24 | loop fusion | flops 4915200 | bytes 4915204 | tf_op jit(solution)/shard_map/jit(_roll_dynamic)/concatenate | solution.py:38
  213.1 1.6 fusion.112
  215.7 2.9 %reshape.538 = bf16[2,2,2,6,25,8,64]{6,5,1,0,4,3,2:T(8,128)(2,1)} reshape(bf16[4,12,25,512]{3,0,2,1:T(4,128)(2,1)S(1)} %copy.194) | data formatting | bytes 2457600 | tf_op jit(solution)/shard_map/reshape | solution.py:51
  218.6 3.7 %copy.195 = bf16[2,2,2,6,25,8,64]{6,5,4,3,2,1,0:T(8,128)(2,1)} copy(bf16[2,2,2,6,25,8,64]{6,5,2,0,4,3,1:T(8,128)(2,1)} %bitcast.118) | data formatting | bytes 2457600 | tf_op jit(solution)/shard_map/transpose | solution.py:54
  223.2 2.7 %reshape.534 = bf16[2,2,2,6,25,8,64]{6,5,1,0,4,3,2:T(8,128)(2,1)} reshape(bf16[4,12,25,512]{3,0,2,1:T(4,128)(2,1)S(1)} %copy.187) | data formatting | bytes 2457600 | tf_op jit(solution)/shard_map/reshape | solution.py:51
  225.9 3.7 %copy.188 = bf16[2,2,2,6,25,8,64]{6,5,4,3,2,1,0:T(8,128)(2,1)} copy(bf16[2,2,2,6,25,8,64]{6,5,2,0,4,3,1:T(8,128)(2,1)} %bitcast.119) | data formatting | bytes 2457600 | tf_op jit(solution)/shard_map/transpose | solution.py:54
  230.6 1.3 copy-done.8
  232.5 5.4 %fusion.38 = bf16[4,36,8,64]{3,1,2,0:T(8,128)(2,1)} fusion(bf16[4,300,8,64]{3,2,1,0:T(8,128)(2,1)} %bitcast.124, f32[4,8,36]{2,1,0:T(8,128)S(1)} %fusion.118, f32[4,8,36,300]{3,2,1,0:T(8,128)} %copy-done.8, pred[4,36,300]{2,1,0:T(8,128)(4,1)S(1)} %copy-done.14), kind=kOutput, calls=%fused_computation.53 | convolution fusion | flops 46039980 | bytes 2806464 | tf_op jit(solution)/shard_map/bhqk,bkhd->bqhd/dot_general | solution.py:84
  237.9 1.1 copy.199
  239.5 2.0 fusion.19
  241.4 2.4 reshape.554
  244.4 1.0 multiply_reduce_fusion
  246.9 1.5 fusion.44
  (135 shorter events, 21.7 us)
Async XLA Ops:
  0.0 239.4 %copy-start = (bf16[512,2048]{1,0:T(8,128)(2,1)S(1)}, bf16[512,2048]{1,0:T(8,128)(2,1)}, u32[]{:S(2)}) copy-start(bf16[512,2048]{1,0:T(8,128)(2,1)} %param.30) | copy-start | bytes 6291460
  0.0 32.3 %copy-start.15 = (s32[2,3]{1,0:T(2,128)S(1)}, s32[2,3]{1,0:T(2,128)}, u32[]{:S(2)}) copy-start(s32[2,3]{1,0:T(2,128)} %param.21) | copy-start | bytes 76
  4.9 56.4 %collective-permute-start.1 = (bf16[4,24,6,512]{3,1,2,0:T(8,128)(2,1)}, bf16[4,24,6,512]{3,1,2,0:T(8,128)(2,1)}, u32[]{:S(2)}, u32[]{:S(2)}) collective-permute-start(bf16[4,24,6,512]{3,1,2,0:T(8,128)(2,1)} %fusion.43), channel_id=1, source_target_pairs={{0,1},{1,2},{2,3},{3,4},{4,5},{5,6},{6,7},{7,8},{8,9},{9,10},{10,1... | collective-permute-start | bytes 1769480 | tf_op jit(solution)/shard_map/ppermute | solution.py:21
  4.9 57.9 %collective-permute-start.2 = (bf16[4,24,6,512]{3,1,2,0:T(8,128)(2,1)}, bf16[4,24,6,512]{3,1,2,0:T(8,128)(2,1)}, u32[]{:S(2)}, u32[]{:S(2)}) collective-permute-start(bf16[4,24,6,512]{3,1,2,0:T(8,128)(2,1)} %fusion.43), channel_id=1, source_target_pairs={{0,127},{1,0},{2,1},{3,2},{4,3},{5,4},{6,5},{7,6},{8,7},{9,8},{10,... | collective-permute-start | bytes 1769480 | tf_op jit(solution)/shard_map/ppermute | solution.py:21
  9.0 51.2 %collective-permute-start = (bf16[4,24,5,512]{3,1,2,0:T(8,128)(2,1)}, bf16[4,24,5,512]{3,1,2,0:T(8,128)(2,1)}, u32[]{:S(2)}, u32[]{:S(2)}) collective-permute-start(bf16[4,24,5,512]{3,1,2,0:T(8,128)(2,1)} %get-tuple-element.16), channel_id=1, source_target_pairs={{0,2},{1,3},{2,4},{3,5},{4,6},{5,7},{6,8},{7,9},{8,10},{9,11},{10,... | collective-permute-start | bytes 1474568 | tf_op jit(solution)/shard_map/ppermute | solution.py:21
  10.6 53.3 %collective-permute-start.3 = (bf16[4,24,5,512]{3,1,2,0:T(8,128)(2,1)}, bf16[4,24,5,512]{3,1,2,0:T(8,128)(2,1)}, u32[]{:S(2)}, u32[]{:S(2)}) collective-permute-start(bf16[4,24,5,512]{3,1,2,0:T(8,128)(2,1)} %get-tuple-element.15), channel_id=1, source_target_pairs={{0,126},{1,127},{2,0},{3,1},{4,2},{5,3},{6,4},{7,5},{8,6},{9,7},{1... | collective-permute-start | bytes 1474568 | tf_op jit(solution)/shard_map/ppermute | solution.py:21
  54.9 4.7 %copy-start.13 = (pred[4,36,300]{2,0,1:T(4,128)(4,1)S(1)}, pred[4,36,300]{2,0,1:T(4,128)(4,1)}, u32[]{:S(2)}) copy-start(pred[4,36,300]{2,0,1:T(4,128)(4,1)} %broadcast_and_fusion.1) | copy-start | bytes 129604
  57.0 5.5 %copy-start.3 = (bf16[4,24,6,512]{3,1,2,0:T(8,128)(2,1)S(1)}, bf16[4,24,6,512]{3,1,2,0:T(8,128)(2,1)}, u32[]{:S(2)}) copy-start(bf16[4,24,6,512]{3,1,2,0:T(8,128)(2,1)} %param.20) | copy-start | bytes 1769476
  57.0 5.5 %copy-start.17 = (f32[512]{0:T(512)S(1)}, f32[512]{0:T(512)}, u32[]{:S(2)}) copy-start(f32[512]{0:T(512)} %param.22) | copy-start | bytes 6148
  61.3 3.7 %copy-start.19 = (bf16[512,1536]{1,0:T(8,128)(2,1)S(1)}, bf16[512,1536]{1,0:T(8,128)(2,1)}, u32[]{:S(2)}) copy-start(bf16[512,1536]{1,0:T(8,128)(2,1)} %param.23) | copy-start | bytes 4718596
  87.6 6.5 %copy-start.1 = (bf16[4,24,28,512]{3,2,1,0:T(8,128)(2,1)S(1)}, bf16[4,24,28,512]{3,2,1,0:T(8,128)(2,1)}, u32[]{:S(2)}) copy-start(bf16[4,24,28,512]{3,2,1,0:T(8,128)(2,1)} %get-tuple-element.6) | copy-start | bytes 8257540
  105.1 4.2 %slice-start = ((s8[5505024]{0:T(1024)(128)(4,1)}), s8[4194304]{0:T(1024)(128)(4,1)S(1)}, s32[]{:S(2)}) async-start(s8[5505024]{0:T(1024)(128)(4,1)} %bitcast.109), calls=%async_computation | async-start | bytes 8388608
  105.1 4.6 %slice-start.1 = ((s8[5505024]{0:T(1024)(128)(4,1)}), s8[1310720]{0:T(1024)(128)(4,1)S(1)}, s32[]{:S(2)}) async-start(s8[5505024]{0:T(1024)(128)(4,1)} %bitcast.109), calls=%async_computation.1 | async-start | bytes 2621440
  105.1 4.6 %copy-start.7 = (bf16[2,4,2,6,6,8,64]{6,5,4,3,2,1,0:T(8,128)(2,1)S(1)}, bf16[2,4,2,6,6,8,64]{6,5,4,3,2,1,0:T(8,128)(2,1)}, u32[]{:S(2)}) copy-start(bf16[2,4,2,6,6,8,64]{6,5,4,3,2,1,0:T(8,128)(2,1)} %copy.165) | copy-start | bytes 1769476
  134.7 1.1 copy-start.5
  138.5 3.7 %copy-start.16 = (f32[2048]{0:T(1024)S(1)}, f32[2048]{0:T(1024)}, u32[]{:S(2)}) copy-start(f32[2048]{0:T(1024)} %param.25) | copy-start | bytes 24580
  142.7 2.8 %copy-start.20 = (bf16[512,1536]{1,0:T(8,128)(2,1)S(1)}, bf16[512,1536]{1,0:T(8,128)(2,1)}, u32[]{:S(2)}) copy-start(bf16[512,1536]{1,0:T(8,128)(2,1)} %param.28) | copy-start | bytes 4718596
  142.7 2.8 %copy-start.21 = (f32[512]{0:T(512)S(1)}, f32[512]{0:T(512)}, u32[]{:S(2)}) copy-start(f32[512]{0:T(512)} %param.27) | copy-start | bytes 6148
  145.2 1.7 copy-start.9
  146.9 35.2 %collective-permute-start.5 = (bf16[4,12,3,1024]{3,1,2,0:T(8,128)(2,1)S(1)}, bf16[4,12,3,1024]{3,1,2,0:T(8,128)(2,1)}, u32[]{:S(2)}, u32[]{:S(2)}) collective-permute-start(bf16[4,12,3,1024]{3,1,2,0:T(8,128)(2,1)S(1)} %slice.107), channel_id=1, source_target_pairs={{0,3},{1,4},{2,5},{3,6},{4,7},{5,8},{6,9},{7,10},{8,11},{9,12},{10... | collective-permute-start | bytes 884744 | tf_op jit(solution)/shard_map/ppermute | solution.py:21
  147.1 40.3 %collective-permute-start.6 = (bf16[4,12,3,1024]{3,1,2,0:T(8,128)(2,1)S(1)}, bf16[4,12,3,1024]{3,1,2,0:T(8,128)(2,1)}, u32[]{:S(2)}, u32[]{:S(2)}) collective-permute-start(bf16[4,12,3,1024]{3,1,2,0:T(8,128)(2,1)S(1)} %slice.107), channel_id=1, source_target_pairs={{0,2},{1,3},{2,4},{3,5},{4,6},{5,7},{6,8},{7,9},{8,10},{9,11},{10,... | collective-permute-start | bytes 884744 | tf_op jit(solution)/shard_map/ppermute | solution.py:21
  147.2 46.7 %collective-permute-start.7 = (bf16[4,12,3,1024]{3,1,2,0:T(8,128)(2,1)S(1)}, bf16[4,12,3,1024]{3,1,2,0:T(8,128)(2,1)}, u32[]{:S(2)}, u32[]{:S(2)}) collective-permute-start(bf16[4,12,3,1024]{3,1,2,0:T(8,128)(2,1)S(1)} %slice.107), channel_id=1, source_target_pairs={{0,1},{1,2},{2,3},{3,4},{4,5},{5,6},{6,7},{7,8},{8,9},{9,10},{10,1... | collective-permute-start | bytes 884744 | tf_op jit(solution)/shard_map/ppermute | solution.py:21
  147.4 47.7 %collective-permute-start.8 = (bf16[4,12,3,1024]{3,1,2,0:T(8,128)(2,1)S(1)}, bf16[4,12,3,1024]{3,1,2,0:T(8,128)(2,1)}, u32[]{:S(2)}, u32[]{:S(2)}) collective-permute-start(bf16[4,12,3,1024]{3,1,2,0:T(8,128)(2,1)S(1)} %slice.107), channel_id=1, source_target_pairs={{0,127},{1,0},{2,1},{3,2},{4,3},{5,4},{6,5},{7,6},{8,7},{9,8},{10,... | collective-permute-start | bytes 884744 | tf_op jit(solution)/shard_map/ppermute | solution.py:21
  149.1 32.1 %collective-permute-start.4 = (bf16[4,12,2,1024]{3,1,2,0:T(8,128)(2,1)}, bf16[4,12,2,1024]{3,1,2,0:T(8,128)(2,1)}, u32[]{:S(2)}, u32[]{:S(2)}) collective-permute-start(bf16[4,12,2,1024]{3,1,2,0:T(8,128)(2,1)} %get-tuple-element.14), channel_id=1, source_target_pairs={{0,4},{1,5},{2,6},{3,7},{4,8},{5,9},{6,10},{7,11},{8,12},{9,13},{1... | collective-permute-start | bytes 589832 | tf_op jit(solution)/shard_map/ppermute | solution.py:21
  181.2 14.9 %collective-permute-start.9 = (bf16[4,12,3,1024]{3,1,2,0:T(8,128)(2,1)S(1)}, bf16[4,12,3,1024]{3,1,2,0:T(8,128)(2,1)S(1)}, u32[]{:S(2)}, u32[]{:S(2)}) collective-permute-start(bf16[4,12,3,1024]{3,1,2,0:T(8,128)(2,1)S(1)} %slice.107), channel_id=1, source_target_pairs={{0,126},{1,127},{2,0},{3,1},{4,2},{5,3},{6,4},{7,5},{8,6},{9,7},{1... | collective-permute-start | bytes 884744 | tf_op jit(solution)/shard_map/ppermute | solution.py:21
  182.2 26.3 %collective-permute-start.10 = (bf16[4,12,3,1024]{3,1,2,0:T(8,128)(2,1)S(1)}, bf16[4,12,3,1024]{3,1,2,0:T(8,128)(2,1)S(1)}, u32[]{:S(2)}, u32[]{:S(2)}) collective-permute-start(bf16[4,12,3,1024]{3,1,2,0:T(8,128)(2,1)S(1)} %slice.107), channel_id=1, source_target_pairs={{0,125},{1,126},{2,127},{3,0},{4,1},{5,2},{6,3},{7,4},{8,5},{9,6},... | collective-permute-start | bytes 884744 | tf_op jit(solution)/shard_map/ppermute | solution.py:21
  187.4 21.1 %collective-permute-start.11 = (bf16[4,12,2,1024]{3,1,2,0:T(8,128)(2,1)}, bf16[4,12,2,1024]{3,1,2,0:T(8,128)(2,1)S(1)}, u32[]{:S(2)}, u32[]{:S(2)}) collective-permute-start(bf16[4,12,2,1024]{3,1,2,0:T(8,128)(2,1)} %get-tuple-element.13), channel_id=1, source_target_pairs={{0,124},{1,125},{2,126},{3,127},{4,0},{5,1},{6,2},{7,3},{8,4},{9,5... | collective-permute-start | bytes 589832 | tf_op jit(solution)/shard_map/ppermute | solution.py:21
  218.6 3.7 %copy-start.4 = (bf16[4,12,25,512]{3,1,2,0:T(8,128)(2,1)S(1)}, bf16[4,12,25,512]{3,1,2,0:T(8,128)(2,1)}, u32[]{:S(2)}) copy-start(bf16[4,12,25,512]{3,1,2,0:T(8,128)(2,1)} %get-tuple-element.12) | copy-start | bytes 3686404
  225.9 3.7 %copy-start.2 = (bf16[2,2,2,6,25,8,64]{6,5,4,3,2,1,0:T(8,128)(2,1)S(1)}, bf16[2,2,2,6,25,8,64]{6,5,4,3,2,1,0:T(8,128)(2,1)}, u32[]{:S(2)}) copy-start(bf16[2,2,2,6,25,8,64]{6,5,4,3,2,1,0:T(8,128)(2,1)} %copy.195) | copy-start | bytes 3686404
  225.9 3.7 %copy-start.11 = (bf16[2,2,2,6,3,8,64]{6,5,4,3,2,1,0:T(8,128)(2,1)S(1)}, bf16[2,2,2,6,3,8,64]{6,5,4,3,2,1,0:T(8,128)(2,1)}, u32[]{:S(2)}) copy-start(bf16[2,2,2,6,3,8,64]{6,5,4,3,2,1,0:T(8,128)(2,1)} %copy.193) | copy-start | bytes 442372
  229.6 2.2 copy-start.14
  230.6 1.3 copy-start.8
  237.9 1.5 copy-start.10
  237.9 1.5 copy-start.12
  241.4 4.2 %copy-start.18 = (f32[512]{0:T(512)S(1)}, f32[512]{0:T(512)}, u32[]{:S(2)}) copy-start(f32[512]{0:T(512)} %param.31) | copy-start | bytes 6148
  245.6 1.3 copy-start.6
where the time goes:
time: 254 us; the launch traced here: 249 us
  local copies, waits for them, and re-layouts  96.8 us (38%)
  waiting for transfers between devices  42.7 us (17%)
  starting transfers between devices  37.3 us (15%)
  other arithmetic  35.8 us (14%)
  matrix products  27.6 us (11%)
  between operations  8.76 us (3%)
    ppermute x12, waiting for transfers between devices, passed_along(): return lax.ppermute(value, axis, pairs)  42.7 us
    ppermute x12, starting transfers between devices, passed_along(): return lax.ppermute(value, axis, pairs)  37.3 us
    reshape x6, local copies, waits for them, and re-layouts, blocked(): tensor_in.reshape(lev_blocks, WIN_LEV, lat_blocks, WIN_LAT, wide_cols, he...  23.3 us
    transpose x6, local copies, waits for them, and re-layouts, blocked(): tensor_in = tensor_in.transpose(0, 2, 1, 3, 4, 5, 6)  21.4 us
    dot_general x2, matrix products, window_attention(): jnp.einsum('bhqk,bkhd->bqhd', weight, value_b, preferred_element_type=jnp...  11.7 us
    unnamed x59, local copies, waits for them, and re-layouts  11.4 us
    concatenate x6, other arithmetic, roll_grid(): jnp.roll(tensor_in, factor * offsets[0], 0)  6.7 us
    concatenate x4, other arithmetic, roll_grid(): jnp.roll(jnp.roll(tensor_in, factor * offsets[0], 0), factor * offsets[1]...  6.42 us
  transfers between devices with their start and end apart: 12, of which 2 were waited for; matrix products, arithmetic and copies ran while one was open for 13% of the time, Pallas kernels for 0%

commit v1 on v0

v1 whole, which is shorter than its diff:
```python
import functools
import math

import jax
import jax.numpy as jnp
from jax import lax
from jax.experimental import pallas as pl
from jax.experimental.pallas import tpu as pltpu
from jax.sharding import PartitionSpec as P

HEADS = 8
WIN_LEV = 2
WIN_LAT = 6
WIN_LON = 12
EPSILON = 1e-05
MASKED = -1e30
MESH = pl.DeviceIdType.MESH
VMEM_LIMIT = 62 * 1024 * 1024


def div(value, by):
    return (value * ((2**20 + by - 1) // by)) >> 20


def iota(shape, dim):
    return lax.broadcasted_iota(jnp.int32, shape, dim)


def one_hot(source, width):
    rows = source.shape[0]
    return (source == iota((rows, width), 1)).astype(jnp.float32).astype(jnp.bfloat16)


def norm(values, gain):
    mean = jnp.mean(values, axis=-1, keepdims=True)
    center = values - mean
    spread = jnp.mean(center * center, axis=-1, keepdims=True)
    return center * lax.rsqrt(spread + EPSILON) * gain


def matmul(left, right):
    return jnp.dot(left, right, preferred_element_type=jnp.float32)


def matmul_nt(left, right):
    return lax.dot_general(
        left, right, (((1,), (1,)), ((), ())), preferred_element_type=jnp.float32
    )


def attend(q_ref, k_ref, v_ref, bias_ref, out_ref):
    rows = q_ref.shape[0]
    width = 128
    head = width // 2
    first = iota((rows, width), 1) < head

    def pair(index, carry):
        lanes = pl.ds(pl.multiple_of(index * width, width), width)
        q = q_ref[:, lanes]
        zero = jnp.zeros_like(q)
        stacked = jnp.concatenate([jnp.where(first, q, zero), jnp.where(first, zero, q)], axis=0)
        scores = matmul_nt(stacked, k_ref[:, lanes])
        bias = bias_ref[...]
        scores = scores + jnp.concatenate([bias, bias], axis=0)
        top = jnp.max(scores, axis=-1, keepdims=True)
        expo = jnp.exp(scores - top)
        total = jnp.sum(expo, axis=-1, keepdims=True)
        mix = matmul(expo.astype(jnp.bfloat16), v_ref[:, lanes]) / total
        out_ref[:, lanes] = jnp.where(first, mix[:rows], mix[rows:]).astype(jnp.bfloat16)
        return carry

    lax.fori_loop(0, q_ref.shape[1] // width, pair, 0)


def roll_kernel(shift_ref, tokens_ref, out_ref, padded):
    levels, lat_rows, cols, features = tokens_ref.shape
    lat_shift = shift_ref[0, 1]
    padded[...] = jnp.zeros_like(padded)
    for level in range(levels):
        padded[level, :, 0:cols, :] = tokens_ref[level].astype(jnp.float32)
    flat = padded[...].reshape(levels * lat_rows * 8, features).astype(jnp.bfloat16)
    group = cols * levels * WIN_LAT
    for window in range(lat_rows // WIN_LAT):
        row = iota((group, 1), 0)
        col = div(row, levels * WIN_LAT)
        rest = row - col * (levels * WIN_LAT)
        level = div(rest, WIN_LAT)
        lat = window * WIN_LAT + rest - level * WIN_LAT - lat_shift
        lat = jnp.where(lat < 0, lat + lat_rows, lat)
        source = (level * lat_rows + lat) * 8 + col
        out_ref[window] = matmul(one_hot(source, flat.shape[0]), flat).astype(jnp.bfloat16)


def main_kernel(
    devices,
    shift_ref,
    x_ref,
    fine_gain_ref,
    merge_gain_ref,
    coarse_gain_ref,
    fine_qkv_hbm,
    fine_proj_hbm,
    merge_hbm,
    coarse_qkv_hbm,
    coarse_proj_hbm,
    fine_out_ref,
    coarse_out_ref,
    fine_qkv,
    fine_proj,
    merge_weight,
    coarse_qkv,
    coarse_proj,
    halo,
    normed,
    q_buf,
    k_buf,
    v_buf,
    bias,
    mix,
    fine_rolled,
    coarse_buf,
    coarse_halo,
    ckey,
    cvalue,
    cbias,
    weight_sem,
    send_sem,
    recv_sem,
    csend_sem,
    crecv_sem,
):
    windows, group, features = x_ref.shape
    levels = 4
    lat_rows = windows * WIN_LAT
    per_col = levels * WIN_LAT
    cols = group // per_col
    part = 128
    me = lax.axis_index("lon")
    parity = lax.rem(me, 2)
    side = 2 * parity - 1
    cgroup = coarse_buf.shape[0]
    ccols = cols // 2
    clat = lat_rows // 2
    cper = levels * clat
    cpart = 2 * cper

    def device(steps):
        return {"lon": lax.rem(me + steps * side + 4 * devices, devices)}

    def weight_copy(index, source, target):
        return pltpu.make_async_copy(source, target, weight_sem.at[index])

    weights = [
        weight_copy(0, fine_qkv_hbm, fine_qkv),
        weight_copy(1, fine_proj_hbm, fine_proj),
        weight_copy(2, merge_hbm, merge_weight),
        weight_copy(3, coarse_qkv_hbm, coarse_qkv),
        weight_copy(4, coarse_proj_hbm, coarse_proj),
    ]
    for copy in weights:
        copy.start()

    barrier = pltpu.get_barrier_semaphore()
    for steps in (1, -1, 2, -2, 3, 4, -4):
        pl.semaphore_signal(barrier, inc=1, device_id=device(steps), device_id_type=MESH)
    pl.semaphore_wait(barrier, 7)

    near = pl.multiple_of(16 * (1 - parity), 16)

    def remote(source, target, kind, index, steps, sends, recvs):
        return pltpu.make_async_remote_copy(
            src_ref=source,
            dst_ref=target,
            send_sem=sends.at[kind, index],
            recv_sem=recvs.at[kind, index],
            device_id=device(steps),
            device_id_type=MESH,
        )

    def fine_copy(kind, w):
        if kind == 0:
            return remote(x_ref.at[w], halo.at[w, pl.ds(0, group)], 0, w, 1, send_sem, recv_sem)
        if kind == 1:
            target = halo.at[w, pl.ds(group, group)]
            return remote(x_ref.at[w], target, 1, w, -1, send_sem, recv_sem)
        if kind == 2:
            target = halo.at[w, pl.ds(2 * group, part)]
            return remote(
                x_ref.at[w, pl.ds(near, part)], target, 2, w, -2, send_sem, recv_sem
            )
        target = halo.at[w, pl.ds(2 * group + part, part)]
        return remote(halo.at[w, pl.ds(near, part)], target, 3, w, -1, send_sem, recv_sem)

    for w in range(windows):
        for kind in range(3):
            fine_copy(kind, w).start()

    lev_shift = shift_ref[0, 0]
    lat_shift = shift_ref[0, 1]
    lon_shift = shift_ref[0, 2] + lax.rem(me * cols, WIN_LON) + 2 * WIN_LON

    def fine_ids(row, steps, w):
        col = div(row, per_col)
        rest = row - col * per_col
        level = div(rest, WIN_LAT)
        lat = rest - level * WIN_LAT
        win = div(col + cols * steps + lon_shift, WIN_LON)
        wrapped = jnp.where(w * lat_rows + lat < lat_shift, 1, 0)
        return (win * 4 + ((level + lev_shift) >> 1)) * 2 + wrapped

    keys = 3 * group + 2 * part
    spot = iota((1, keys), 1)
    slot = div(spot, group)
    row = spot - slot * group
    steps = jnp.where(slot == 0, 0, jnp.where(slot == 1, side, -side))
    far_out = (spot >= 3 * group) & (spot < 3 * group + part)
    far_in = spot >= 3 * group + part
    steps = jnp.where(far_out, 2 * side, jnp.where(far_in, -2 * side, steps))
    row = jnp.where(far_out, spot - 3 * group, jnp.where(far_in, spot - 3 * group - part, row))
    row = jnp.where((spot >= 3 * group) & (steps < 0), row + 16, row)
    gain = fine_gain_ref[...]

    weights[0].wait()

    def fine_kv(start, size):
        piece = normed[pl.ds(start, size), :]
        kv = matmul(piece, fine_qkv[:, features:])
        k_buf[pl.ds(start, size), :] = kv[:, :features].astype(jnp.bfloat16)
        v_buf[pl.ds(start, size), :] = kv[:, features:].astype(jnp.bfloat16)

    def fine_window(w, carry):
        own = x_ref[w]
        query_id = fine_ids(iota((group, 1), 0), 0, w)
        key_id = fine_ids(row, steps, w)
        bias[...] = jnp.where(query_id == key_id, 0.0, MASKED)
        normed[0:group, :] = norm(own.astype(jnp.float32), gain).astype(jnp.bfloat16)
        q = matmul(normed[0:group, :], fine_qkv[:, :features]).astype(jnp.bfloat16)
        q_buf[...] = q * jnp.bfloat16(1.0 / math.sqrt(features // HEADS))
        fine_copy(0, w).wait_recv()
        fine_copy(3, w).start()
        fine_copy(1, w).wait_recv()
        normed[group : 3 * group, :] = norm(
            halo[w, 0 : 2 * group, :].astype(jnp.float32), gain
        ).astype(jnp.bfloat16)
        fine_kv(0, 3 * group)
        fine_copy(2, w).wait_recv()
        fine_copy(3, w).wait_recv()
        normed[3 * group :, :] = norm(
            halo[w, 2 * group :, :].astype(jnp.float32), gain
        ).astype(jnp.bfloat16)
        fine_kv(3 * group, 2 * part)
        attend(q_buf, k_buf, v_buf, bias, mix)
        update = matmul(mix[...], fine_proj[...])
        fine_rolled[pl.ds(pl.multiple_of(w * group, 16), group), :] = (
            own.astype(jnp.float32) + update
        ).astype(jnp.bfloat16)
        return carry

    weights[1].wait()
    lax.fori_loop(0, windows, fine_window, 0)

    crow = iota((cgroup, 1), 0)
    ccol = div(crow, cper)
    rest = crow - ccol * cper
    clevel = div(rest, clat)
    clat_row = rest - clevel * clat
    fine_all = fine_rolled[...]
    total = jnp.zeros((cgroup, 1), jnp.float32)
    pieces = []
    for piece in range(4):
        lat = 2 * clat_row + piece % 2 + lat_shift
        lat = jnp.where(lat >= lat_rows, lat - lat_rows, lat)
        window = div(lat, WIN_LAT)
        source = (
            window * group
            + (2 * ccol + piece // 2) * per_col
            + clevel * WIN_LAT
            + lat
            - window * WIN_LAT
        )
        picked = matmul(one_hot(source, windows * group), fine_all)
        fine_out_ref[piece] = picked.astype(jnp.bfloat16)
        pieces.append(picked)
        total = total + jnp.sum(picked, axis=-1, keepdims=True)
    mean = total / (4 * features)
    square = jnp.zeros((cgroup, 1), jnp.float32)
    for piece in range(4):
        pieces[piece] = pieces[piece] - mean
        square = square + jnp.sum(pieces[piece] * pieces[piece], axis=-1, keepdims=True)
    scale = lax.rsqrt(square / (4 * features) + EPSILON)
    weights[2].wait()
    coarse = jnp.zeros((cgroup, features), jnp.float32)
    for piece in range(4):
        merged = pieces[piece] * scale * merge_gain_ref[pl.ds(piece, 1), :]
        coarse = coarse + matmul(
            merged.astype(jnp.bfloat16), merge_weight[pl.ds(piece * features, features), :]
        )
    coarse_buf[...] = coarse.astype(jnp.bfloat16)

    clev_shift = shift_ref[1, 0]
    clat_shift = shift_ref[1, 1]
    clon_shift = shift_ref[1, 2] + lax.rem(me * ccols, WIN_LON) + 2 * WIN_LON

    def coarse_ids(row, steps):
        col = div(row, cper)
        rest = row - col * cper
        level = div(rest, clat)
        lat = rest - level * clat
        win = div(col + ccols * steps + clon_shift, WIN_LON)
        return (win * 4 + ((level + clev_shift) >> 1)) * 4 + div(lat + clat_shift, WIN_LAT)

    ckeys = 7 * cgroup + 2 * cpart
    spot = iota((1, ckeys), 1)
    slot = div(spot, cgroup)
    crow = spot - slot * cgroup
    csteps = jnp.zeros_like(spot)
    for number, amount in enumerate((0, 1, -1, 2, 3, -2, -3)):
        csteps = jnp.where(slot == number, amount * side, csteps)
    far_out = (spot >= 7 * cgroup) & (spot < 7 * cgroup + cpart)
    far_in = spot >= 7 * cgroup + cpart
    csteps = jnp.where(far_out, 4 * side, jnp.where(far_in, -4 * side, csteps))
    crow = jnp.where(
        far_out, spot - 7 * cgroup, jnp.where(far_in, spot - 7 * cgroup - cpart, crow)
    )
    crow = jnp.where((spot >= 7 * cgroup) & (csteps < 0), crow + cper, crow)
    query_id = coarse_ids(iota((cgroup, 1), 0), 0)
    cbias[...] = jnp.where(query_id == coarse_ids(crow, csteps), 0.0, MASKED)

    cnear = pl.multiple_of(cper * (1 - parity), 16)
    starts = {1: 0, -1: cgroup, 2: 2 * cgroup, 3: 3 * cgroup, -2: 4 * cgroup, -3: 5 * cgroup}
    starts[4] = 6 * cgroup
    starts[-4] = 6 * cgroup + cpart

    def coarse_remote(kind, source, slot, size, steps):
        return remote(
            source, coarse_halo.at[pl.ds(starts[slot], size)], kind, 0, steps, csend_sem, crecv_sem
        )

    whole = coarse_buf
    ccopies = {
        1: coarse_remote(0, whole, 1, cgroup, 1),
        -1: coarse_remote(1, whole, -1, cgroup, -1),
        2: coarse_remote(2, whole, 2, cgroup, -2),
        3: coarse_remote(3, whole, 3, cgroup, 3),
        4: coarse_remote(4, whole.at[pl.ds(cnear, cpart)], 4, cpart, -4),
        -2: coarse_remote(5, coarse_halo.at[pl.ds(starts[1], cgroup)], -2, cgroup, -1),
        -3: coarse_remote(6, coarse_halo.at[pl.ds(starts[2], cgroup)], -3, cgroup, -1),
        -4: coarse_remote(
            7, coarse_halo.at[pl.ds(pl.multiple_of(starts[3] + cnear, 16), cpart)], -4, cpart, -1
        ),
    }
    for slot in (1, 2, 3, 4, -1):
        ccopies[slot].start()

    cgain = coarse_gain_ref[...]
    weights[3].wait()

    def coarse_kv(values, start, size):
        piece = norm(values.astype(jnp.float32), cgain).astype(jnp.bfloat16)
        kv = matmul(piece, coarse_qkv[:, features:])
        ckey[pl.ds(start, size), :] = kv[:, :features].astype(jnp.bfloat16)
        cvalue[pl.ds(start, size), :] = kv[:, features:].astype(jnp.bfloat16)
        return piece

    piece = coarse_kv(coarse_buf[...], 0, cgroup)
    q = matmul(piece, coarse_qkv[:, :features]).astype(jnp.bfloat16)
    q_buf[...] = q * jnp.bfloat16(1.0 / math.sqrt(features // HEADS))
    for slot, relay in ((-1, None), (1, -2), (2, -3), (3, -4), (-2, None), (-3, None), (4, None), (-4, None)):
        ccopies[slot].wait_recv()
        if relay is not None:
            ccopies[relay].start()
        size = cpart if abs(slot) == 4 else cgroup
        coarse_kv(coarse_halo[pl.ds(starts[slot], size), :], cgroup + starts[slot], size)
    attend(q_buf, ckey, cvalue, cbias, mix)
    weights[4].wait()
    update = matmul(mix[...], coarse_proj[...])
    coarse_out_ref[...] = (coarse_buf[...].astype(jnp.float32) + update).astype(jnp.bfloat16)

    for slot in (1, -1, 2, 3, 4, -2, -3, -4):
        ccopies[slot].wait_send()
    for w in range(windows):
        for kind in range(4):
            fine_copy(kind, w).wait_send()


def expand_kernel(fine_ref, coarse_ref, weight_ref, gain_ref, out_ref, joined):
    levels, lat_rows, cols, features = out_ref.shape
    group = coarse_ref.shape[0]
    clat = lat_rows // 2
    cper = levels * clat
    gain = gain_ref[...]
    coarse = coarse_ref[...]
    for piece in range(4):
        expanded = matmul(coarse, weight_ref[:, piece * features : (piece + 1) * features])
        joined[piece * group : (piece + 1) * group, :] = (
            fine_ref[piece].astype(jnp.float32) + norm(expanded, gain)
        ).astype(jnp.bfloat16)
    pieces = joined[...]
    row = iota((lat_rows * 8, 1), 0)
    lat = row >> 3
    col = row & 7
    for level in range(levels):
        source = (
            (2 * (col & 1) + (lat & 1)) * group + (col >> 1) * cper + level * clat + (lat >> 1)
        )
        source = jnp.where(col < cols, source, -1)
        picked = matmul(one_hot(source, 4 * group), pieces)
        picked = picked.reshape(lat_rows, 8, features)[:, :cols, :]
        out_ref[level] = picked.astype(jnp.bfloat16)


def local(
    tokens,
    window_shift,
    fine_gain,
    fine_qkv,
    fine_proj,
    merge_gain,
    merge_weight,
    coarse_gain,
    coarse_qkv,
    coarse_proj,
    expand_weight,
    expand_gain,
):
    devices = lax.axis_size("lon")
    levels, lat_rows, cols, features = tokens.shape
    windows = lat_rows // WIN_LAT
    group = cols * levels * WIN_LAT
    cgroup = levels * (lat_rows // 2) * (cols // 2)
    cpart = 2 * levels * (lat_rows // 2)
    part = 128
    keys = 3 * group + 2 * part
    ckeys = 7 * cgroup + 2 * cpart
    bf16 = jnp.bfloat16
    vmem = pl.BlockSpec(memory_space=pltpu.VMEM)
    smem = pl.BlockSpec(memory_space=pltpu.SMEM)
    anywhere = pl.BlockSpec(memory_space=pl.ANY)
    rolled = pl.pallas_call(
        roll_kernel,
        out_shape=jax.ShapeDtypeStruct((windows, group, features), bf16),
        in_specs=[smem, vmem],
        out_specs=vmem,
        scratch_shapes=[pltpu.VMEM((levels, lat_rows, 8, features), jnp.float32)],
        compiler_params=pltpu.CompilerParams(vmem_limit_bytes=VMEM_LIMIT),
        name="roll",
    )(window_shift, tokens)
    fine, coarse = pl.pallas_call(
        functools.partial(main_kernel, devices),
        out_shape=(
            jax.ShapeDtypeStruct((4, cgroup, features), bf16),
            jax.ShapeDtypeStruct((cgroup, features), bf16),
        ),
        in_specs=[smem] + [vmem] * 4 + [anywhere] * 5,
        out_specs=(vmem, vmem),
        scratch_shapes=[
            pltpu.VMEM(fine_qkv.shape, bf16),
            pltpu.VMEM(fine_proj.shape, bf16),
            pltpu.VMEM(merge_weight.shape, bf16),
            pltpu.VMEM(coarse_qkv.shape, bf16),
            pltpu.VMEM(coarse_proj.shape, bf16),
            pltpu.VMEM((windows, keys - group, features), bf16),
            pltpu.VMEM((keys, features), bf16),
            pltpu.VMEM((group, features), bf16),
            pltpu.VMEM((keys, features), bf16),
            pltpu.VMEM((keys, features), bf16),
            pltpu.VMEM((group, keys), jnp.float32),
            pltpu.VMEM((group, features), bf16),
            pltpu.VMEM((windows * group, features), bf16),
            pltpu.VMEM((cgroup, features), bf16),
            pltpu.VMEM((ckeys - cgroup, features), bf16),
            pltpu.VMEM((ckeys, features), bf16),
            pltpu.VMEM((ckeys, features), bf16),
            pltpu.VMEM((cgroup, ckeys), jnp.float32),
            pltpu.SemaphoreType.DMA((5,)),
            pltpu.SemaphoreType.DMA((4, windows)),
            pltpu.SemaphoreType.DMA((4, windows)),
            pltpu.SemaphoreType.DMA((8, 1)),
            pltpu.SemaphoreType.DMA((8, 1)),
        ],
        compiler_params=pltpu.CompilerParams(
            collective_id=0, has_side_effects=True, vmem_limit_bytes=VMEM_LIMIT
        ),
        name="encode",
    )(
        window_shift,
        rolled,
        fine_gain.reshape(1, features),
        merge_gain.reshape(4, features),
        coarse_gain.reshape(1, features),
        fine_qkv,
        fine_proj,
        merge_weight,
        coarse_qkv,
        coarse_proj,
    )
    return pl.pallas_call(
        expand_kernel,
        out_shape=jax.ShapeDtypeStruct(tokens.shape, tokens.dtype),
        in_specs=[vmem] * 4,
        out_specs=vmem,
        scratch_shapes=[pltpu.VMEM((4 * cgroup, features), bf16)],
        compiler_params=pltpu.CompilerParams(vmem_limit_bytes=VMEM_LIMIT),
        name="expand",
    )(fine, coarse, expand_weight, expand_gain.reshape(1, features))


def solution(mesh):
    placed = (P("groups", None, "lon", None), P(), P(), P(), P(), P(), P(), P(), P(), P(), P(), P())
    return jax.shard_map(
        local, mesh=mesh, in_specs=placed, out_specs=P("groups", None, "lon", None), check_vma=False
    )
```

time: 254 us -> 88.9 us (0.35)
  the two profiles are of different devices: /device:TPU:34 before, /device:TPU:33 now
where the time goes in v1:
time: 88.9 us; the launch traced here: 88.6 us
  Pallas kernels  83 us (93%)
  local copies, waits for them, and re-layouts  5.56 us (6%)
    pallas_call x1, Pallas kernels, local(): pl.pallas_call(functools.partial(main_kernel, devices), out_shape=(jax.Sh...  76 us
    pallas_call x1, Pallas kernels, local(): pl.pallas_call(expand_kernel, out_shape=jax.ShapeDtypeStruct(tokens.shape...  4.24 us
    pallas_call x1, Pallas kernels, local(): pl.pallas_call(roll_kernel, out_shape=jax.ShapeDtypeStruct((windows, grou...  2.83 us
    unnamed x1, local copies, waits for them, and re-layouts  2.14 us
    pallas_call x1, local copies, waits for them, and re-layouts, local(): pl.pallas_call(expand_kernel, out_shape=jax.ShapeDtypeStruct(tokens.shape...  2.13 us

profile of v1, /device:TPU:33, one launch (start us, length us, event | category | flops | bytes accessed | tf_op | source)
XLA Modules:
  0.0 88.6 jit_solution(8557710612005985090)
XLA Ops:
  0.0 1.3 %reshape.13.merge_gain_ref = f32[4,512]{1,0:T(4,128)} reshape(f32[2048]{0:T(1024)} %param.17) | data formatting | bytes 16384 | tf_op jit(solution)/shard_map/reshape | solution.py:489
  1.3 2.1 %copy.13.tokens_ref = bf16[4,24,6,512]{3,2,1,0:T(8,128)(2,1)} copy(bf16[4,24,6,512]{3,1,2,0:T(8,128)(2,1)} %param.12) | data formatting | bytes 1179648 | tf_op args[0]
  3.4 2.8 %roll.1.x_ref = bf16[4,144,512]{2,1,0:T(8,128)(2,1)} custom-call(s32[2,3]{1,0:T(2,128)} %shift_ref.3, bf16[4,24,6,512]{3,2,1,0:T(8,128)(2,1)} %copy.13.tokens_ref), custom_call_target="tpu_custom_call" | custom-call | tf_op jit(solution)/shard_map/roll/pallas_call | solution.py:439
  6.3 76.0 %encode.1 = (bf16[4,144,512]{2,1,0:T(8,128)(2,1)}, bf16[144,512]{1,0:T(8,128)(2,1)}) custom-call(s32[2,3]{1,0:T(2,128)} %shift_ref.3, bf16[4,144,512]{2,1,0:T(8,128)(2,1)} %roll.1.x_ref, f32[1,512]{1,0:T(1,128)} %bitcast.3, f32[4,512]{1,0:T(4,128)} %reshape.13.merge_gain_ref, f32[1,512]{1,0:T(1,128)} %bitcast.4, bf16[512,1536]{1,0:T(8,128)(2,1)} %fine_qkv_hbm.1, ...), custom_call_target="tpu_custom_call" | custom-call | tf_op jit(solution)/shard_map/encode/pallas_call | solution.py:448
  82.2 4.2 %expand.1 = bf16[4,24,6,512]{3,2,1,0:T(8,128)(2,1)} custom-call(bf16[4,144,512]{2,1,0:T(8,128)(2,1)} %get-tuple-element.7.fine_ref, bf16[144,512]{1,0:T(8,128)(2,1)} %get-tuple-element.8.coarse_ref, bf16[512,2048]{1,0:T(8,128)(2,1)} %weight_ref.1, f32[1,512]{1,0:T(1,128)} %bitcast.5), custom_call_target="tpu_custom_call" | custom-call | tf_op jit(solution)/shard_map/expand/pallas_call | solution.py:497
  86.5 2.1 %copy.14 = bf16[4,24,6,512]{3,1,2,0:T(8,128)(2,1)} copy(bf16[4,24,6,512]{3,2,1,0:T(8,128)(2,1)} %expand.1) | data formatting | bytes 1179648 | tf_op jit(solution)/shard_map/expand/pallas_call | solution.py:497
